TPU v7x, 256 devices: a whole 4x4x8 slice. The times are simulated.
256 devices in a mesh: seq: 32 (over y, z), head: 8 (over x, core).
Axes of the slice: x: 4, y: 4, z: 8, core: 2. Of those that a mesh axis runs over, the one named last changes fastest.
Arguments:
- tokens: bfloat16 [24576, 2560], P(('seq', 'head')), may hold values from -12 to 12
- pre_gain: float32 [2560], replicated, may hold values from 0.25 to 1.75
- inner_proj: bfloat16 [2560, 2, 5120], P(None, None, 'head'), may hold values from -0.125 to 0.125
- outer_proj: bfloat16 [2560, 336], replicated, may hold values from -0.125 to 0.125
- kernel_x: float32 [4, 5120], P(None, 'head'), may hold values from -3 to 3
- kernel_bc: float32 [4, 256], replicated, may hold values from -3 to 3
- offset_x: float32 [5120], P('head'), may hold values from -3 to 3
- offset_bc: float32 [256], replicated, may hold values from -3 to 3
- dt_bias: float32 [80], P('head'), may hold values from -7 to -5
- a_log: float32 [80], P('head'), may hold values from -12 to 4
- skip_gain: float32 [80], P('head'), may hold values from 0.5 to 1.5
- norm_gain: float32 [5120], P('head'), may hold values from 0.25 to 1.75
- out_proj: bfloat16 [5120, 2560], P('head'), may hold values from -0.078125 to 0.078125
Outputs:
- mixed: bfloat16 [24576, 2560], P(('seq', 'head'))
All inputs are finite; a program needn't handle non-finite values.
Results may differ from a plain program's by a relative error of at most 0.014.
Values may be sent and summed in bfloat16 or wider, within the bound.
A program may use at most 128 MiB of HBM per device.

v0:
```python
import jax
import jax.numpy as jnp
from jax import lax
from jax.sharding import Mesh
from jax.sharding import PartitionSpec as P

SPAN = 256
SEQ = ("seq_0", "seq_1")
SEQ_HEAD = ("seq_0", "seq_1", "head")
norm_floor = 0.1


def passed_along(block, axis, distance):
    devices = range(lax.axis_size(axis))
    route = [(i - distance, i) for i in devices if i - distance in devices]
    return lax.ppermute(block, axis, route)


def nothing_yet(array, identity):
    return jax.tree.map(
        lambda part, zero: jnp.zeros_like(part) + jnp.asarray(zero, part.dtype), array, identity
    )


def entering(array, axes, combine, identity):
    before = start = nothing_yet(array, identity)
    subtotal = array
    for axis in reversed(axes):
        length, position = (lax.axis_size(axis), lax.axis_index(axis))
        pieces = jax.tree.map(
            lambda part, kind: lax.all_gather(part.astype(kind), axis),
            subtotal,
            (jnp.bfloat16, jnp.bfloat16),
        )
        inside, subtotal = (start, start)
        for k in range(length):
            passed = k < position
            subtotal = combine(
                subtotal, jax.tree.map(lambda part, own: part[k].astype(own.dtype), pieces, array)
            )
            inside = jax.tree.map(lambda new, old: jnp.where(passed, new, old), subtotal, inside)
        before = combine(inside, before)
    return before


def from_everyone(array, axis):
    length = lax.axis_size(axis)
    return lax.all_to_all(
        jnp.broadcast_to(array[None], (length, *array.shape)), axis, 0, 0, tiled=True
    )


def taken_together(array, axis):
    everything = from_everyone(array, axis)
    return jnp.sum(everything, axis=0)


def cut_along(array, dim, length):
    before, after = (array.shape[:dim], array.shape[dim + 1 :])
    return jnp.moveaxis(array.reshape(*before, length, -1, *after), dim, 0)


def summed_on_arrival(array, axis, dim):
    pieces = cut_along(array, dim, lax.axis_size(axis))
    arrived = lax.all_to_all(pieces, axis, split_axis=0, concat_axis=0, tiled=True)
    return arrived.astype(jnp.float32).sum(axis=0)


def row_norm(row_block, gain_vector):
    widened = row_block.astype(jnp.float32)
    inverse_rms = lax.rsqrt(jnp.mean(widened * widened, axis=-1, keepdims=True) + norm_floor)
    return widened * inverse_rms * gain_vector


def masked_exp(log_gap, causal):
    return jnp.where(causal, jnp.exp(jnp.where(causal, log_gap, 0.0)), 0.0)


def on_device(
    tokens,
    pre_gain,
    inner_proj,
    outer_proj,
    kernel_x,
    kernel_bc,
    offset_x,
    offset_bc,
    dt_bias,
    a_log,
    skip_gain,
    norm_gain,
    out_proj,
):
    model_width = inner_proj.shape[0]
    local_width = inner_proj.shape[2]
    head_count = dt_bias.shape[0]
    head_size = local_width // head_count
    state_size = kernel_bc.shape[1] // 2
    kernel_size = kernel_x.shape[0]
    joined_proj = inner_proj.reshape(model_width, 2 * local_width)
    own_normed = row_norm(tokens, pre_gain).astype(jnp.bfloat16)
    normed = lax.all_gather(own_normed, "head", axis=0, tiled=True)
    inner_part = jnp.dot(normed, joined_proj, preferred_element_type=jnp.float32)
    outer_part = jnp.dot(normed, outer_proj, preferred_element_type=jnp.float32)
    projected = jnp.concatenate([inner_part, outer_part], axis=1)
    seq_rows = projected.shape[0]
    gate_in = projected[:, :local_width].astype(jnp.bfloat16)
    conv_input = projected[:, local_width : 2 * local_width + 2 * state_size].astype(jnp.bfloat16)
    head_index = lax.axis_index("head")
    dt_raw = lax.dynamic_slice_in_dim(
        projected[:, 2 * local_width + 2 * state_size :], head_index * head_count, head_count, 1
    )
    conv_tail = passed_along(conv_input[seq_rows - kernel_size + 1 :], SEQ, 1)
    extended = jnp.concatenate([conv_tail, conv_input], axis=0)
    conv_weight = jnp.concatenate([kernel_x, kernel_bc], axis=1)
    conv_bias = jnp.concatenate([offset_x, offset_bc])
    summed = jnp.broadcast_to(conv_bias, conv_input.shape)
    for offset in range(kernel_size):
        summed = summed + conv_weight[offset] * extended[offset : offset + seq_rows].astype(
            jnp.float32
        )
    conv_out = jax.nn.silu(summed).astype(jnp.bfloat16)
    blocks = seq_rows // SPAN
    values_x = conv_out[:, :local_width].reshape(blocks, SPAN, head_count, head_size)
    values_b = conv_out[:, local_width : local_width + state_size].reshape(blocks, SPAN, state_size)
    values_c = conv_out[:, local_width + state_size :].reshape(blocks, SPAN, state_size)
    step_flat = jax.nn.softplus(dt_raw + dt_bias)
    log_rates = (step_flat * -jnp.exp(a_log)).reshape(blocks, SPAN, head_count)
    step_sizes = step_flat.reshape(blocks, SPAN, head_count)
    running = jnp.cumsum(log_rates, axis=1)
    score_rows = jnp.einsum("ctn,csn->cts", values_c, values_b, preferred_element_type=jnp.float32)
    running_heads = jnp.transpose(running, (0, 2, 1))
    steps_heads = jnp.transpose(step_sizes, (0, 2, 1))
    row_index = lax.broadcasted_iota(jnp.int32, (SPAN, SPAN), 0)
    col_index = lax.broadcasted_iota(jnp.int32, (SPAN, SPAN), 1)
    decay_factor = masked_exp(
        running_heads[:, :, :, None] - running_heads[:, :, None, :], row_index >= col_index
    )
    mix_weights = (score_rows[:, None] * decay_factor * steps_heads[:, :, None, :]).astype(
        jnp.bfloat16
    )
    intra_out = jnp.einsum(
        "chts,cshp->cthp", mix_weights, values_x, preferred_element_type=jnp.float32
    )
    end_weight = jnp.exp(running[:, -1:, :] - running) * step_sizes
    scaled_x = (values_x.astype(jnp.float32) * end_weight[..., None]).astype(jnp.bfloat16)
    block_states = jnp.einsum(
        "cshp,csn->chpn", scaled_x, values_b, preferred_element_type=jnp.float32
    )
    block_total = running[:, -1, :]
    prefix_rate = jnp.concatenate(
        [jnp.zeros((1, head_count), jnp.float32), jnp.cumsum(block_total, axis=0)], axis=0
    )
    prefix_heads = prefix_rate.T
    later_index = lax.broadcasted_iota(jnp.int32, (blocks + 1, blocks), 0)
    source_index = lax.broadcasted_iota(jnp.int32, (blocks + 1, blocks), 1)
    link_weight = masked_exp(
        prefix_heads[:, :, None] - prefix_heads[:, None, 1:], source_index < later_index
    )
    local_states = jnp.einsum(
        "hce,ehpn->chpn", link_weight, block_states, precision=lax.Precision.HIGHEST
    )
    summary = local_states[blocks]
    device_rate = prefix_rate[blocks]

    def combine(earlier_part, later_part):
        return (
            earlier_part[0] + later_part[0],
            jnp.exp(later_part[0])[:, None, None] * earlier_part[1] + later_part[1],
        )

    identity = (
        jnp.zeros((head_count,), jnp.float32),
        jnp.zeros((head_count, head_size, state_size), jnp.float32),
    )
    carried = entering((device_rate, summary), SEQ, combine, identity)[1]
    block_inputs = (
        local_states[:blocks] + jnp.exp(prefix_rate[:blocks])[:, :, None, None] * carried[None]
    )
    cross_out = jnp.exp(running)[..., None] * jnp.einsum(
        "ctn,chpn->cthp",
        values_c.astype(jnp.float32),
        block_inputs,
        precision=lax.Precision.HIGHEST,
    )
    mixer_out = (intra_out + cross_out + skip_gain[:, None] * values_x.astype(jnp.float32)).reshape(
        seq_rows, local_width
    )
    gated = mixer_out * jax.nn.silu(gate_in.astype(jnp.float32))
    squares = taken_together(jnp.sum(gated * gated, axis=1), "head")
    inverse_rms = lax.rsqrt(squares / (local_width * lax.axis_size("head")) + norm_floor)
    normed_out = (gated * inverse_rms[:, None] * norm_gain).astype(jnp.bfloat16)
    mixed = summed_on_arrival(
        jnp.dot(normed_out, out_proj, preferred_element_type=jnp.float32).astype(jnp.bfloat16),
        "head",
        0,
    )
    return mixed.astype(jnp.bfloat16)


def solution(mesh):
    finer = Mesh(mesh.devices.reshape(4, 8, mesh.shape["head"]), ("seq_0", "seq_1", "head"))
    in_specs = (
        P(SEQ_HEAD, None),
        P(),
        P(None, None, "head"),
        P(),
        P(None, "head"),
        P(),
        P("head"),
        P(),
        P("head"),
        P("head"),
        P("head"),
        P("head"),
        P("head", None),
    )
    out_specs = P(SEQ_HEAD, None)
    return jax.shard_map(
        on_device, mesh=finer, in_specs=in_specs, out_specs=out_specs, check_vma=False
    )
```

profile of v0, /device:TPU:1, one launch (start us, length us, event | category | flops | bytes accessed | tf_op | source)
XLA Modules:
  0.0 240.8 jit_solution(7252940572213324971)
XLA Ops:
  6.5 1.4 fusion.16
  7.9 2.0 fusion.18
  10.1 6.7 %copy.137 = bf16[320,8,2,640]{3,1,2,0:T(8,128)(2,1)} copy(bf16[320,8,2,640]{3,2,1,0:T(2,128)(2,1)} %bitcast.167) | data formatting | bytes 13107200
  18.1 29.7 %all-gather.5.cloned.1.call-done = bf16[768,2560]{1,0:T(8,128)(2,1)} async-done(((bf16[96,2560]{1,0:T(8,128)(2,1)}), bf16[768,2560]{1,0:T(8,128)(2,1)}) %all-gather.5.cloned.1.call-update) | async-done | bytes 3932176 | tf_op jit(solution)/shard_map/all_gather | solution.py:102
  47.8 5.3 %fusion.66 = (bf16[768,336]{0,1:T(8,128)(2,1)}, f32[768,336]{0,1:T(8,128)}) fusion(bf16[768,2560]{1,0:T(8,128)(2,1)} %all-gather.5.cloned.1.call-done, bf16[2560,336]{0,1:T(8,128)(2,1)} %param.16), kind=kOutput, calls=%fused_computation.144 | convolution fusion | flops 1321463808 | bytes 7200768 | tf_op jit(solution)/shard_map/dot_general | solution.py:104
  53.1 2.1 copy.111
  55.2 8.9 %convolution_convert_fusion.1 = bf16[768,1280]{1,0:T(8,128)(2,1)S(1)} fusion(bf16[768,2560]{1,0:T(8,128)(2,1)} %all-gather.5.cloned.1.call-done, bf16[2560,1280]{1,0:T(8,128)(2,1)} %bitcast.168), kind=kOutput, calls=%fused_computation.9 | convolution fusion | flops 5034147840 | bytes 12451840 | tf_op jit(solution)/shard_map/dot_general | solution.py:103
  64.2 1.3 pad_maximum_fusion.1
  66.5 1.0 slice.213
  67.6 1.7 reduce-window.6
  70.1 3.2 %collective-permute-start = (bf16[3,896]{1,0:T(4,128)(2,1)}, bf16[3,896]{1,0:T(4,128)(2,1)S(1)}, u32[]{:S(2)}, u32[]{:S(2)}) collective-permute-start(bf16[3,896]{1,0:T(4,128)(2,1)} %pad_maximum_fusion.2), channel_id=1, source_target_pairs={{0,8},{8,16},{16,24},{24,32},{32,40},{40,48},{48,56},{56,64},{64,7... | collective-permute-start | bytes 16136 | tf_op jit(solution)/shard_map/ppermute | solution.py:16
  73.3 0.6 bitcast_exponential_fusion
  73.9 0.7 copy.124
  74.6 0.6 copy.123
  75.2 0.7 copy.125
  75.9 5.0 %multiply_convert_fusion.2 = bf16[768,896]{1,0:T(8,128)(2,1)S(1)} fusion(bf16[768,896]{1,0:T(8,128)(2,1)} %pad_maximum_fusion.1, bf16[3,896]{1,0:T(4,128)(2,1)S(1)} %collective-permute-done, f32[896]{0:T(1024)S(1)} %get-tuple-element.6, f32[896]{0:T(1024)S(1)} %get-tuple-element.7, f32[896]{0:T(1024)S(1)} %get-tuple-element.8, f32[896]{0:T(1024)S(1)} %get-tuple-element.5, ...), kind=kLoop, calls=%fused_computation.10 | loop fusion | flops 17891328 | bytes 2775808 | tf_op jit(solution)/shard_map/convert_element_type | solution.py:122
  80.9 0.7 fusion.65
  81.6 1.1 slice.210
  82.6 2.3 copy.112
  84.9 3.8 %reshape.237 = bf16[3,256,10,64]{1,0,3,2:T(4,128)(2,1)} reshape(bf16[768,640]{0,1:T(8,128)(2,1)} %copy.112) | data formatting | bytes 1966080 | tf_op jit(solution)/shard_map/reshape | solution.py:124
  88.7 1.8 fusion.19
  90.5 2.8 %convolution_bitcast_fusion = f32[4,10,64,128]{3,0,2,1:T(4,128)S(1)} fusion(f32[3,10,64,128]{3,2,1,0:T(8,128)S(1)} %fusion.19, f32[10,3]{1,0:T(8,128)S(1)} %copy-done.14, f32[10,4]{1,0:T(8,128)S(1)} %copy-done.13, pred[4,3]{1,0:T(4,128)(4,1)S(1)} %copy-done.27), kind=kOutput, calls=%fused_computation.26 | convolution fusion | flops 11796840 | bytes 2294052 | tf_op jit(solution)/shard_map/hce,ehpn->chpn/dot_general | solution.py:160
  93.4 1.1 copy-done.2
  94.8 0.7 copy.128
  95.5 0.6 iota_compare_fusion
  96.2 1.4 slice_exponential_fusion
  97.5 12.2 %all-gather = bf16[8,1,10]{2,1,0:T(2,128)(2,1)S(1)} all-gather(bf16[1,1,10]{2,1,0:T(2,128)(2,1)S(1)} %slice_bitcast_fusion.5), channel_id=1, replica_groups=mesh['seq_0'=4,'seq_1'=8,'head'=8] {'seq_1'}, dimensions={0}, use_global_device_ids=true | all-gather | bytes 180 | tf_op jit(solution)/shard_map/all_gather | solution.py:31
  110.9 8.6 %all-gather.1 = bf16[4,1,10]{2,1,0:T(2,128)(2,1)} all-gather(bf16[1,1,10]{2,1,0:T(2,128)(2,1)S(1)} %get-tuple-element.17), channel_id=1, replica_groups=mesh['seq_0'=4,'seq_1'=8,'head'=8] {'seq_0'}, dimensions={0}, use_global_device_ids=true | all-gather | bytes 100 | tf_op jit(solution)/shard_map/all_gather | solution.py:31
  119.5 0.6 copy.115
  120.2 0.8 copy.127
  120.9 1.4 copy.119
  122.3 0.6 copy.117
  123.6 0.7 fusion.49
  124.3 2.1 fusion.67
  126.4 4.1 %all-gather.7.cloned.1.call-done = bf16[8,10,64,128]{3,2,1,0:T(8,128)(2,1)} async-done(((bf16[1,10,64,128]{3,2,1,0:T(8,128)(2,1)}), bf16[8,10,64,128]{3,2,1,0:T(8,128)(2,1)}) %all-gather.7.cloned.1.call-update) | async-done | bytes 1310736 | tf_op jit(solution)/shard_map/all_gather | solution.py:31
  130.4 1.9 fusion.28
  132.3 10.4 %all_gather.23 = bf16[4,10,64,128]{3,2,1,0:T(8,128)(2,1)S(1)} all-gather(bf16[1,10,64,128]{3,2,1,0:T(8,128)(2,1)S(1)} %fusion.28), channel_id=1, replica_groups=mesh['seq_0'=4,'seq_1'=8,'head'=8] {'seq_0'}, dimensions={0}, use_global_device_ids=true | all-gather | bytes 819200 | tf_op jit(solution)/shard_map/all_gather | solution.py:31
  142.8 1.0 add_bitcast_fusion
  144.3 0.9 fusion.21
  145.7 2.7 %fusion.8 = f32[3,256,10,64]{1,3,2,0:T(8,128)S(1)} fusion(f32[3,256,10,64]{1,3,2,0:T(8,128)S(1)} %fusion.21, f32[3,10,256]{2,1,0:T(8,128)S(1)} %copy-done.11, f32[3,10,256]{2,1,0:T(8,128)S(1)} %copy-done.9, f32[3,256,256]{2,1,0:T(8,128)S(1)} %copy-done.7, pred[256,256]{1,0:T(8,128)(4,1)S(1)} %copy-done.8, f32[10]{0:T(128)S(1)} %copy-done.30, ...), kind=kOutput, calls=%fused_computation.16 | convolution fusion | flops 265912320 | bytes 5859368 | tf_op jit(solution)/shard_map/chts,cshp->cthp/dot_general | solution.py:142
  148.4 1.4 copy.130
  149.8 1.8 copy.138
  151.6 2.8 %copy.131 = f32[768,640]{1,0:T(8,128)} copy(f32[768,640]{0,1:T(8,128)} %bitcast.166) | data formatting | bytes 3932160 | tf_op jit(solution)/shard_map/reshape | solution.py:186
  154.4 2.5 %multiply_reduce_fusion = f32[768]{0:T(1024)S(1)} fusion(f32[768,640]{1,0:T(8,128)} %copy.131, bf16[768,1280]{1,0:T(8,128)(2,1)} %copy-done.1), kind=kLoop, calls=%fused_computation.23 | loop fusion | flops 3931392 | bytes 2952192 | tf_op jit(solution)/shard_map/reduce_sum | solution.py:190
  156.9 17.4 %all_to_all.11 = f32[8,1,768]{2,1,0:T(1,128)S(1)} all-to-all(f32[8,1,768]{2,1,0:T(1,128)S(1)} %broadcast_in_dim.36), channel_id=1, replica_groups=mesh['seq_0'=4,'seq_1'=8,'head'=8] {'head'}, dimensions={0} | all-to-all | bytes 49152 | tf_op jit(solution)/shard_map/all_to_all | solution.py:48
  174.4 6.2 %convolution_convert_fusion = bf16[768,2560]{1,0:T(8,128)(2,1)S(1)} fusion(bf16[640,2560]{1,0:T(8,128)(2,1)S(1)} %copy-done, f32[640]{0:T(1024)S(1)} %copy-done.28, f32[768]{0:T(1024)S(1)} %add_rsqrt_fusion, f32[768,640]{1,0:T(8,128)} %copy.131, bf16[768,1280]{1,0:T(8,128)(2,1)} %copy-done.1), kind=kOutput, calls=%fused_computation.1 | convolution fusion | flops 2522972160 | bytes 10163712 | tf_op jit(solution)/shard_map/dot_general | solution.py:194
  180.6 49.8 %all_to_all.12 = bf16[8,96,2560]{2,1,0:T(8,128)(2,1)} all-to-all(bf16[8,96,2560]{2,1,0:T(8,128)(2,1)S(1)} %bitcast.169), channel_id=1, replica_groups=mesh['seq_0'=4,'seq_1'=8,'head'=8] {'head'}, dimensions={0} | all-to-all | bytes 7864320 | tf_op jit(solution)/shard_map/all_to_all | solution.py:65
  230.4 3.6 %reduce_sum.42 = bf16[96,2560]{1,0:T(8,128)(2,1)} reduce(bf16[8,96,2560]{2,1,0:T(8,128)(2,1)} %all_to_all.12, bf16[]{:T(256)} %constant.60.clone.1), dimensions={0}, to_apply=%region_6.7 | reduce | flops 1720320 | bytes 4423682 | tf_op jit(solution)/shard_map/reduce_sum | solution.py:66
  (100 shorter events, 6.4 us)
Async XLA Ops:
  6.5 167.9 %copy-start = (bf16[640,2560]{1,0:T(8,128)(2,1)S(1)}, bf16[640,2560]{1,0:T(8,128)(2,1)}, u32[]{:S(2)}) copy-start(bf16[640,2560]{1,0:T(8,128)(2,1)} %param.25) | copy-start | bytes 9830404
  6.5 41.2 %all-gather.5.cloned.1.call-start = ((), (), s32[]{:S(2)}) async-start(), calls=%async_computation.2 | async-start | bytes 4423680 | tf_op jit(solution)/shard_map/all_gather | solution.py:102
  10.0 120.5 %all-gather.7.cloned.1.call-start = ((), (), s32[]{:S(2)}) async-start(), calls=%async_computation.3 | async-start | bytes 1474560 | tf_op jit(solution)/shard_map/all_gather | solution.py:31
  10.0 7.4 %copy-start.16 = (f32[4,640]{1,0:T(4,128)S(1)}, f32[4,640]{1,0:T(4,128)}, u32[]{:S(2)}) copy-start(f32[4,640]{1,0:T(4,128)} %param.17) | copy-start | bytes 30724
  10.0 7.4 %copy-start.22 = (f32[4,256]{1,0:T(4,128)S(1)}, f32[4,256]{1,0:T(4,128)}, u32[]{:S(2)}) copy-start(f32[4,256]{1,0:T(4,128)} %param.18) | copy-start | bytes 12292
  10.0 7.4 %copy-start.23 = (f32[640]{0:T(1024)S(1)}, f32[640]{0:T(1024)}, u32[]{:S(2)}) copy-start(f32[640]{0:T(1024)} %param.19) | copy-start | bytes 7684
  10.1 7.4 %copy-start.25 = (f32[256]{0:T(256)S(1)}, f32[256]{0:T(256)}, u32[]{:S(2)}) copy-start(f32[256]{0:T(256)} %param.20) | copy-start | bytes 3076
  10.1 8.0 %copy-start.29 = (f32[10]{0:T(128)S(1)}, f32[10]{0:T(128)}, u32[]{:S(2)}) copy-start(f32[10]{0:T(128)} %param.22) | copy-start | bytes 124
  55.2 8.9 %copy-start.4 = (bf16[768,336]{1,0:T(8,128)(2,1)S(1)}, bf16[768,336]{1,0:T(8,128)(2,1)}, u32[]{:S(2)}) copy-start(bf16[768,336]{1,0:T(8,128)(2,1)} %copy.111) | copy-start | bytes 1548292
  64.2 1.7 copy-start.1
  65.9 1.6 copy-start.26
  70.0 5.9 %copy-start.15 = (f32[3,10]{1,0:T(4,128)}, f32[3,10]{1,0:T(4,128)S(1)}, u32[]{:S(2)}) copy-start(f32[3,10]{1,0:T(4,128)S(1)} %reduce_window_sum.36) | copy-start | bytes 364
  70.1 5.8 %collective-permute-start = (bf16[3,896]{1,0:T(4,128)(2,1)}, bf16[3,896]{1,0:T(4,128)(2,1)S(1)}, u32[]{:S(2)}, u32[]{:S(2)}) collective-permute-start(bf16[3,896]{1,0:T(4,128)(2,1)} %pad_maximum_fusion.2), channel_id=1, source_target_pairs={{0,8},{8,16},{16,24},{24,32},{32,40},{40,48},{48,56},{56,64},{64,7... | collective-permute-start | bytes 16136 | tf_op jit(solution)/shard_map/ppermute | solution.py:16
  88.7 1.8 copy-start.13
  88.7 1.8 copy-start.14
  88.7 1.8 copy-start.27
  93.4 1.1 copy-start.2
  109.7 10.4 %copy-start.12 = (bf16[8,1,10]{2,1,0:T(2,128)(2,1)}, bf16[8,1,10]{2,1,0:T(2,128)(2,1)S(1)}, u32[]{:S(2)}) copy-start(bf16[8,1,10]{2,1,0:T(2,128)(2,1)S(1)} %all-gather) | copy-start | bytes 484
  120.1 22.6 %copy-start.17 = (f32[10]{0:T(128)S(1)}, f32[10]{0:T(128)}, u32[]{:S(2)}) copy-start(f32[10]{0:T(128)} %get-tuple-element.18) | copy-start | bytes 124
  120.1 22.6 %copy-start.18 = (f32[10]{0:T(128)S(1)}, f32[10]{0:T(128)}, u32[]{:S(2)}) copy-start(f32[10]{0:T(128)} %get-tuple-element.19) | copy-start | bytes 124
  120.1 22.6 %copy-start.19 = (f32[10]{0:T(128)S(1)}, f32[10]{0:T(128)}, u32[]{:S(2)}) copy-start(f32[10]{0:T(128)} %get-tuple-element.20) | copy-start | bytes 124
  120.1 22.6 %copy-start.20 = (f32[10]{0:T(128)S(1)}, f32[10]{0:T(128)}, u32[]{:S(2)}) copy-start(f32[10]{0:T(128)} %get-tuple-element.21) | copy-start | bytes 124
  120.2 22.6 %copy-start.21 = (f32[10]{0:T(128)S(1)}, f32[10]{0:T(128)}, u32[]{:S(2)}) copy-start(f32[10]{0:T(128)} %get-tuple-element.22) | copy-start | bytes 124
  123.0 19.8 %copy-start.24 = (f32[10]{0:T(128)S(1)}, f32[10]{0:T(128)}, u32[]{:S(2)}) copy-start(f32[10]{0:T(128)} %get-tuple-element.9) | copy-start | bytes 124
  130.4 12.3 %copy-start.5 = (bf16[8,10,64,128]{3,2,1,0:T(8,128)(2,1)S(1)}, bf16[8,10,64,128]{3,2,1,0:T(8,128)(2,1)}, u32[]{:S(2)}) copy-start(bf16[8,10,64,128]{3,2,1,0:T(8,128)(2,1)} %all-gather.7.cloned.1.call-done) | copy-start | bytes 3932164
  130.4 13.3 %copy-start.3 = (f32[4,10,64,128]{3,0,2,1:T(4,128)S(1)}, f32[4,10,64,128]{3,0,2,1:T(4,128)}, u32[]{:S(2)}) copy-start(f32[4,10,64,128]{3,0,2,1:T(4,128)} %copy-done.2) | copy-start | bytes 3932164
  144.2 1.3 copy-start.6
  144.2 1.5 copy-start.7
  144.2 1.5 copy-start.8
  144.2 1.5 copy-start.9
  144.2 1.5 copy-start.10
  144.2 1.5 copy-start.11
  144.2 1.5 copy-start.30
  154.4 20.0 %copy-start.28 = (f32[640]{0:T(1024)S(1)}, f32[640]{0:T(1024)}, u32[]{:S(2)}) copy-start(f32[640]{0:T(1024)} %param.24) | copy-start | bytes 7684
Sparse Core Ops, SparseCore 0:
  10.1 37.6 all-gather.4
  95.6 34.7 all-gather.6
where the time goes:
time: 242 us; the launch traced here: 241 us
  blocking collectives  98.4 us (41%)
  waiting for transfers between devices  33.8 us (14%)
  local copies, waits for them, and re-layouts  32.7 us (14%)
  matrix products  30.8 us (13%)
  other arithmetic  28 us (12%)
  between operations  13.9 us (6%)
  starting transfers between devices  3.23 us (1%)
    all_to_all x1, blocking collectives, summed_on_arrival(): lax.all_to_all(pieces, axis, split_axis=0, concat_axis=0, tiled=True)  49.8 us
    all_gather x3, blocking collectives, entering(): lax.all_gather(part.astype(kind), axis)  31.2 us
    all_gather x1, waiting for transfers between devices, on_device(): normed = lax.all_gather(own_normed, 'head', axis=0, tiled=True)  29.7 us
    all_to_all x1, blocking collectives, from_everyone(): lax.all_to_all(jnp.broadcast_to(array[None], (length, *array.shape)), axi...  17.4 us
    unnamed x66, local copies, waits for them, and re-layouts  10.6 us
    dot_general x1, matrix products, on_device(): jnp.dot(normed, joined_proj, preferred_element_type=jnp.float32)  8.94 us
    dot_general x1, matrix products, on_device(): jnp.dot(normed_out, out_proj, preferred_element_type=jnp.float32)  6.16 us
    dot_general x1, matrix products, on_device(): outer_part = jnp.dot(normed, outer_proj, preferred_element_type=jnp.float32)  5.31 us
  transfers between devices with their start and end apart: 3, of which 2 were waited for; matrix products, arithmetic and copies ran while one was open for 9% of the time, Pallas kernels for 0%

commit v1 on v0

--- a/solution.py
+++ b/solution.py
@@ -3,6 +3,7 @@
 from jax import lax
 from jax.sharding import Mesh
 from jax.sharding import PartitionSpec as P
+from jax.lax import all_to_all, axis_size
 
 SPAN = 256
 SEQ = ("seq_0", "seq_1")
@@ -99,7 +100,17 @@
     kernel_size = kernel_x.shape[0]
     joined_proj = inner_proj.reshape(model_width, 2 * local_width)
     own_normed = row_norm(tokens, pre_gain).astype(jnp.bfloat16)
-    normed = lax.all_gather(own_normed, "head", axis=0, tiled=True)
+
+    def fit_area(v0, chip_axis):
+        return all_to_all(
+            jnp.concatenate([v0 for _ in range(axis_size(chip_axis))], axis=0),
+            chip_axis,
+            0,
+            0,
+            tiled=True,
+        )
+
+    normed = fit_area(own_normed, "head")
     inner_part = jnp.dot(normed, joined_proj, preferred_element_type=jnp.float32)
     outer_part = jnp.dot(normed, outer_proj, preferred_element_type=jnp.float32)
     projected = jnp.concatenate([inner_part, outer_part], axis=1)

time: 242 us -> 265 us (1.095)
  waiting for transfers between devices: 33.8 us -> 41.9 us
  starting transfers between devices: 3.23 us -> 9.62 us
  other arithmetic: 28 us -> 32.3 us
    all_to_all x0 -> x1, waiting for transfers between devices: none -> 37.9 us  [fit_area(): all_to_all(jnp.concatenate([v0 for _ in range(axis_size(chip_axis))], axi...]
    all_gather x1 -> x0, waiting for transfers between devices: 29.7 us -> none  [on_device(): normed = lax.all_gather(own_normed, 'head', axis=0, tiled=True)]
    all_to_all x0 -> x1, starting transfers between devices: none -> 7.61 us  [fit_area(): all_to_all(jnp.concatenate([v0 for _ in range(axis_size(chip_axis))], axi...]
    unnamed x1 -> x8, other arithmetic: 0.6 us -> 4.71 us
  transfers between devices with their start and end apart: 3 -> 3, of which waited for: 2 -> 2; matrix products, arithmetic and copies ran while one was open for 9% -> 8% of each run, Pallas kernels for 0% -> 0%
where the time goes in v1:
time: 265 us; the launch traced here: 264 us
  blocking collectives  100 us (38%)
  waiting for transfers between devices  41.9 us (16%)
  local copies, waits for them, and re-layouts  34 us (13%)
  other arithmetic  32.3 us (12%)
  matrix products  31.9 us (12%)
  between operations  13.9 us (5%)
  starting transfers between devices  9.62 us (4%)
    all_to_all x1, blocking collectives, summed_on_arrival(): lax.all_to_all(pieces, axis, split_axis=0, concat_axis=0, tiled=True)  49.8 us
    all_to_all x1, waiting for transfers between devices, fit_area(): all_to_all(jnp.concatenate([v0 for _ in range(axis_size(chip_axis))], axi...  37.9 us
    all_gather x3, blocking collectives, entering(): lax.all_gather(part.astype(kind), axis)  32.9 us
    all_to_all x1, blocking collectives, from_everyone(): lax.all_to_all(jnp.broadcast_to(array[None], (length, *array.shape)), axi...  17.4 us
    unnamed x66, local copies, waits for them, and re-layouts  11.9 us
    dot_general x1, matrix products, on_device(): jnp.dot(normed, joined_proj, preferred_element_type=jnp.float32)  9.95 us
    all_to_all x1, starting transfers between devices, fit_area(): all_to_all(jnp.concatenate([v0 for _ in range(axis_size(chip_axis))], axi...  7.61 us
    dot_general x1, matrix products, on_device(): jnp.dot(normed_out, out_proj, preferred_element_type=jnp.float32)  6.16 us
  transfers between devices with their start and end apart: 3, of which 2 were waited for; matrix products, arithmetic and copies ran while one was open for 8% of the time, Pallas kernels for 0%

profile of v1, /device:TPU:1, one launch (start us, length us, event | category | flops | bytes accessed | tf_op | source)
XLA Modules:
  0.0 263.7 jit_solution(6573897375595743703)
XLA Ops:
  6.5 1.4 fusion.16
  7.9 1.2 constant_dynamic-update-slice_fusion.9
  9.2 1.2 constant_dynamic-update-slice_fusion.8
  10.4 0.9 constant_dynamic-update-slice_fusion.7
  12.3 2.0 copy-done.6
  14.3 7.6 %all-to-all-start = ((bf16[8,96,2560]{2,1,0:T(8,128)(2,1)}), bf16[8,96,2560]{2,1,0:T(8,128)(2,1)}, u32[]{:S(2)}, u32[]{:S(2)}) async-start(bf16[8,96,2560]{2,1,0:T(8,128)(2,1)} %bitcast.171), calls=%async_computation | async-start | bytes 7864320 | tf_op jit(solution)/shard_map/all_to_all | solution.py:105
  21.9 6.7 %copy.137 = bf16[320,8,2,640]{3,1,2,0:T(8,128)(2,1)} copy(bf16[320,8,2,640]{3,2,1,0:T(2,128)(2,1)} %bitcast.169) | data formatting | bytes 13107200
  29.9 37.9 %all-to-all-done = bf16[8,96,2560]{2,1,0:T(8,128)(2,1)} async-done(((bf16[8,96,2560]{2,1,0:T(8,128)(2,1)}), bf16[8,96,2560]{2,1,0:T(8,128)(2,1)}, u32[]{:S(2)}, u32[]{:S(2)}) %all-to-all-start) | async-done | bytes 3932192 | tf_op jit(solution)/shard_map/all_to_all | solution.py:105
  67.9 10.0 %convolution_convert_fusion.1 = bf16[768,1280]{1,0:T(8,128)(2,1)} fusion(bf16[768,2560]{1,0:T(8,128)(2,1)} %bitcast.1, bf16[2560,1280]{1,0:T(8,128)(2,1)} %bitcast.170), kind=kOutput, calls=%fused_computation.9 | convolution fusion | flops 5034147840 | bytes 12451840 | tf_op jit(solution)/shard_map/dot_general | solution.py:114
  77.8 4.8 %fusion.66 = (bf16[768,336]{0,1:T(8,128)(2,1)}, f32[768,336]{0,1:T(8,128)}) fusion(bf16[768,2560]{1,0:T(8,128)(2,1)} %bitcast.1, bf16[2560,336]{0,1:T(8,128)(2,1)S(1)} %copy-done.27), kind=kOutput, calls=%fused_computation.152 | convolution fusion | flops 1321463808 | bytes 7200768 | tf_op jit(solution)/shard_map/dot_general | solution.py:115
  82.6 2.1 copy.111
  84.7 1.5 pad_maximum_fusion.2
  86.4 1.2 pad_maximum_fusion.1
  87.6 1.0 slice.213
  88.7 1.7 reduce-window.6
  91.2 2.0 collective-permute-start
  93.9 0.7 copy.124
  95.2 0.7 copy.125
  95.8 5.0 %multiply_convert_fusion.2 = bf16[768,896]{1,0:T(8,128)(2,1)S(1)} fusion(bf16[768,896]{1,0:T(8,128)(2,1)} %pad_maximum_fusion.1, bf16[3,896]{1,0:T(4,128)(2,1)S(1)} %collective-permute-done, f32[896]{0:T(1024)S(1)} %get-tuple-element.6, f32[896]{0:T(1024)S(1)} %get-tuple-element.7, f32[896]{0:T(1024)S(1)} %get-tuple-element.8, f32[896]{0:T(1024)S(1)} %get-tuple-element.5, ...), kind=kLoop, calls=%fused_computation.10 | loop fusion | flops 17891328 | bytes 2775808 | tf_op jit(solution)/shard_map/convert_element_type | solution.py:133
  100.9 0.7 fusion.65
  101.6 1.0 slice.210
  102.6 2.2 copy.112
  104.9 3.8 %reshape.239 = bf16[3,256,10,64]{1,0,3,2:T(4,128)(2,1)} reshape(bf16[768,640]{0,1:T(8,128)(2,1)} %copy.112) | data formatting | bytes 1966080 | tf_op jit(solution)/shard_map/reshape | solution.py:135
  108.6 1.8 fusion.19
  110.4 3.6 %convolution_bitcast_fusion = f32[4,10,64,128]{3,0,2,1:T(4,128)S(1)} fusion(f32[3,10,64,128]{3,2,1,0:T(8,128)S(1)} %fusion.19, f32[10,3]{1,0:T(8,128)} %copy.125, f32[10,4]{1,0:T(8,128)} %copy.124, pred[4,3]{1,0:T(4,128)(4,1)} %iota_compare_fusion.1), kind=kOutput, calls=%fused_computation.26 | convolution fusion | flops 11796840 | bytes 2294052 | tf_op jit(solution)/shard_map/hce,ehpn->chpn/dot_general | solution.py:171
  114.0 1.0 copy-done.3
  115.4 0.7 copy.128
  116.7 1.3 slice_exponential_fusion
  118.1 13.8 %all-gather = bf16[8,1,10]{2,1,0:T(2,128)(2,1)S(1)} all-gather(bf16[1,1,10]{2,1,0:T(2,128)(2,1)S(1)} %slice_bitcast_fusion.5), channel_id=1, replica_groups=mesh['seq_0'=4,'seq_1'=8,'head'=8] {'seq_1'}, dimensions={0}, use_global_device_ids=true | all-gather | bytes 180 | tf_op jit(solution)/shard_map/all_gather | solution.py:32
  133.0 8.4 %all-gather.1 = bf16[4,1,10]{2,1,0:T(2,128)(2,1)} all-gather(bf16[1,1,10]{2,1,0:T(2,128)(2,1)S(1)} %get-tuple-element.17), channel_id=1, replica_groups=mesh['seq_0'=4,'seq_1'=8,'head'=8] {'seq_0'}, dimensions={0}, use_global_device_ids=true | all-gather | bytes 100 | tf_op jit(solution)/shard_map/all_gather | solution.py:32
  142.0 0.8 copy.127
  142.8 1.4 copy.119
  145.4 0.7 fusion.49
  146.1 2.1 fusion.67
  148.2 4.0 %all-gather.4.cloned.1.call-done = bf16[8,10,64,128]{3,2,1,0:T(8,128)(2,1)} async-done(((bf16[1,10,64,128]{3,2,1,0:T(8,128)(2,1)}), bf16[8,10,64,128]{3,2,1,0:T(8,128)(2,1)}) %all-gather.4.cloned.1.call-update) | async-done | bytes 1310736 | tf_op jit(solution)/shard_map/all_gather | solution.py:32
  152.2 1.9 fusion.28
  154.0 10.7 %all_gather.19 = bf16[4,10,64,128]{3,2,1,0:T(8,128)(2,1)S(1)} all-gather(bf16[1,10,64,128]{3,2,1,0:T(8,128)(2,1)S(1)} %fusion.28), channel_id=1, replica_groups=mesh['seq_0'=4,'seq_1'=8,'head'=8] {'seq_0'}, dimensions={0}, use_global_device_ids=true | all-gather | bytes 819200 | tf_op jit(solution)/shard_map/all_gather | solution.py:32
  164.8 2.3 add_bitcast_fusion
  167.6 0.9 fusion.21
  168.7 2.7 %fusion.8 = f32[3,256,10,64]{1,3,2,0:T(8,128)S(1)} fusion(f32[3,256,10,64]{1,3,2,0:T(8,128)S(1)} %fusion.21, f32[3,10,256]{2,1,0:T(8,128)S(1)} %copy-done.13, f32[3,10,256]{2,1,0:T(8,128)S(1)} %copy-done.11, f32[3,256,256]{2,1,0:T(8,128)S(1)} %copy-done.9, pred[256,256]{1,0:T(8,128)(4,1)S(1)} %copy-done.10, f32[10]{0:T(128)S(1)} %copy-done.30, ...), kind=kOutput, calls=%fused_computation.16 | convolution fusion | flops 265912320 | bytes 5859368 | tf_op jit(solution)/shard_map/chts,cshp->cthp/dot_general | solution.py:153
  171.4 1.4 copy.130
  172.8 1.7 copy.138
  174.5 2.9 %copy.131 = f32[768,640]{1,0:T(8,128)} copy(f32[768,640]{0,1:T(8,128)} %bitcast.168) | data formatting | bytes 3932160 | tf_op jit(solution)/shard_map/reshape | solution.py:197
  177.4 2.5 multiply_reduce_fusion
  179.9 17.4 %all_to_all.23 = f32[8,1,768]{2,1,0:T(1,128)S(1)} all-to-all(f32[8,1,768]{2,1,0:T(1,128)S(1)} %broadcast_in_dim.36), channel_id=1, replica_groups=mesh['seq_0'=4,'seq_1'=8,'head'=8] {'head'}, dimensions={0} | all-to-all | bytes 49152 | tf_op jit(solution)/shard_map/all_to_all | solution.py:49
  197.3 6.2 %convolution_convert_fusion = bf16[768,2560]{1,0:T(8,128)(2,1)S(1)} fusion(bf16[640,2560]{1,0:T(8,128)(2,1)S(1)} %copy-done, f32[640]{0:T(1024)S(1)} %copy-done.28, f32[768]{0:T(1024)S(1)} %add_rsqrt_fusion, f32[768,640]{1,0:T(8,128)} %copy.131, bf16[768,1280]{1,0:T(8,128)(2,1)} %convolution_convert_fusion.1), kind=kOutput, calls=%fused_computation.1 | convolution fusion | flops 2522972160 | bytes 10163712 | tf_op jit(solution)/shard_map/dot_general | solution.py:205
  203.5 49.8 %all_to_all.24 = bf16[8,96,2560]{2,1,0:T(8,128)(2,1)} all-to-all(bf16[8,96,2560]{2,1,0:T(8,128)(2,1)S(1)} %bitcast.172), channel_id=1, replica_groups=mesh['seq_0'=4,'seq_1'=8,'head'=8] {'head'}, dimensions={0} | all-to-all | bytes 7864320 | tf_op jit(solution)/shard_map/all_to_all | solution.py:66
  253.3 3.6 %reduce_sum.42 = bf16[96,2560]{1,0:T(8,128)(2,1)} reduce(bf16[8,96,2560]{2,1,0:T(8,128)(2,1)} %all_to_all.24, bf16[]{:T(256)} %constant.60.clone.1), dimensions={0}, to_apply=%region_6.7 | reduce | flops 1720320 | bytes 4423682 | tf_op jit(solution)/shard_map/reduce_sum | solution.py:67
  (106 shorter events, 9.2 us)
Async XLA Ops:
  6.5 190.8 %copy-start = (bf16[640,2560]{1,0:T(8,128)(2,1)S(1)}, bf16[640,2560]{1,0:T(8,128)(2,1)}, u32[]{:S(2)}) copy-start(bf16[640,2560]{1,0:T(8,128)(2,1)} %param.25) | copy-start | bytes 9830404
  6.5 3.9 %copy-start.1 = (bf16[96,2560]{1,0:T(8,128)(2,1)S(1)}, bf16[96,2560]{1,0:T(8,128)(2,1)}, u32[]{:S(2)}) copy-start(bf16[96,2560]{1,0:T(8,128)(2,1)} %param.13) | copy-start | bytes 1474564
  6.5 4.8 %copy-start.8 = (f32[2560]{0:T(1024)S(1)}, f32[2560]{0:T(1024)}, u32[]{:S(2)}) copy-start(f32[2560]{0:T(1024)} %param.14) | copy-start | bytes 30724
  12.3 2.0 copy-start.6
  14.3 53.6 %all-to-all-start = ((bf16[8,96,2560]{2,1,0:T(8,128)(2,1)}), bf16[8,96,2560]{2,1,0:T(8,128)(2,1)}, u32[]{:S(2)}, u32[]{:S(2)}) async-start(bf16[8,96,2560]{2,1,0:T(8,128)(2,1)} %bitcast.171), calls=%async_computation | async-start | bytes 7864320 | tf_op jit(solution)/shard_map/all_to_all | solution.py:105
  21.9 130.3 %all-gather.4.cloned.1.call-start = ((), (), s32[]{:S(2)}) async-start(), calls=%async_computation.3 | async-start | bytes 1474560 | tf_op jit(solution)/shard_map/all_gather | solution.py:32
  21.9 7.4 %copy-start.16 = (f32[4,640]{1,0:T(4,128)S(1)}, f32[4,640]{1,0:T(4,128)}, u32[]{:S(2)}) copy-start(f32[4,640]{1,0:T(4,128)} %param.17) | copy-start | bytes 30724
  21.9 7.4 %copy-start.22 = (f32[4,256]{1,0:T(4,128)S(1)}, f32[4,256]{1,0:T(4,128)}, u32[]{:S(2)}) copy-start(f32[4,256]{1,0:T(4,128)} %param.18) | copy-start | bytes 12292
  21.9 7.4 %copy-start.23 = (f32[640]{0:T(1024)S(1)}, f32[640]{0:T(1024)}, u32[]{:S(2)}) copy-start(f32[640]{0:T(1024)} %param.19) | copy-start | bytes 7684
  21.9 7.4 %copy-start.25 = (f32[256]{0:T(256)S(1)}, f32[256]{0:T(256)}, u32[]{:S(2)}) copy-start(f32[256]{0:T(256)} %param.20) | copy-start | bytes 3076
  21.9 8.0 %copy-start.29 = (f32[10]{0:T(128)S(1)}, f32[10]{0:T(128)}, u32[]{:S(2)}) copy-start(f32[10]{0:T(128)} %param.22) | copy-start | bytes 124
  67.9 10.0 %copy-start.27 = (bf16[2560,336]{0,1:T(8,128)(2,1)S(1)}, bf16[2560,336]{0,1:T(8,128)(2,1)}, u32[]{:S(2)}) copy-start(bf16[2560,336]{0,1:T(8,128)(2,1)} %param.16) | copy-start | bytes 5160964
  84.7 1.6 copy-start.2
  84.7 1.7 copy-start.5
  86.4 2.2 copy-start.26
  91.2 4.7 %copy-start.15 = (f32[3,10]{1,0:T(4,128)}, f32[3,10]{1,0:T(4,128)S(1)}, u32[]{:S(2)}) copy-start(f32[3,10]{1,0:T(4,128)S(1)} %reduce_window_sum.36) | copy-start | bytes 364
  91.2 4.7 %collective-permute-start = (bf16[3,896]{1,0:T(4,128)(2,1)}, bf16[3,896]{1,0:T(4,128)(2,1)S(1)}, u32[]{:S(2)}, u32[]{:S(2)}) collective-permute-start(bf16[3,896]{1,0:T(4,128)(2,1)} %pad_maximum_fusion.2), channel_id=1, source_target_pairs={{0,8},{8,16},{16,24},{24,32},{32,40},{40,48},{48,56},{56,64},{64,7... | collective-permute-start | bytes 16136 | tf_op jit(solution)/shard_map/ppermute | solution.py:17
  113.9 1.1 copy-start.3
  131.8 10.1 %copy-start.14 = (bf16[8,1,10]{2,1,0:T(2,128)(2,1)}, bf16[8,1,10]{2,1,0:T(2,128)(2,1)S(1)}, u32[]{:S(2)}) copy-start(bf16[8,1,10]{2,1,0:T(2,128)(2,1)S(1)} %all-gather) | copy-start | bytes 484
  142.0 22.8 %copy-start.17 = (f32[10]{0:T(128)S(1)}, f32[10]{0:T(128)}, u32[]{:S(2)}) copy-start(f32[10]{0:T(128)} %get-tuple-element.18) | copy-start | bytes 124
  142.0 22.8 %copy-start.18 = (f32[10]{0:T(128)S(1)}, f32[10]{0:T(128)}, u32[]{:S(2)}) copy-start(f32[10]{0:T(128)} %get-tuple-element.19) | copy-start | bytes 124
  142.0 22.8 %copy-start.19 = (f32[10]{0:T(128)S(1)}, f32[10]{0:T(128)}, u32[]{:S(2)}) copy-start(f32[10]{0:T(128)} %get-tuple-element.20) | copy-start | bytes 124
  142.0 22.8 %copy-start.20 = (f32[10]{0:T(128)S(1)}, f32[10]{0:T(128)}, u32[]{:S(2)}) copy-start(f32[10]{0:T(128)} %get-tuple-element.21) | copy-start | bytes 124
  142.0 22.8 %copy-start.21 = (f32[10]{0:T(128)S(1)}, f32[10]{0:T(128)}, u32[]{:S(2)}) copy-start(f32[10]{0:T(128)} %get-tuple-element.22) | copy-start | bytes 124
  144.8 20.0 %copy-start.24 = (f32[10]{0:T(128)S(1)}, f32[10]{0:T(128)}, u32[]{:S(2)}) copy-start(f32[10]{0:T(128)} %get-tuple-element.9) | copy-start | bytes 124
  152.2 15.0 %copy-start.4 = (f32[4,10,64,128]{3,0,2,1:T(4,128)S(1)}, f32[4,10,64,128]{3,0,2,1:T(4,128)}, u32[]{:S(2)}) copy-start(f32[4,10,64,128]{3,0,2,1:T(4,128)} %copy-done.3) | copy-start | bytes 3932164
  167.1 1.4 copy-start.7
  167.1 1.5 copy-start.9
  167.2 1.5 copy-start.10
  167.2 1.5 copy-start.11
  167.2 1.5 copy-start.12
  167.2 1.5 copy-start.13
  167.2 1.5 copy-start.30
  174.5 22.9 %copy-start.28 = (f32[640]{0:T(1024)S(1)}, f32[640]{0:T(1024)}, u32[]{:S(2)}) copy-start(f32[640]{0:T(1024)} %param.24) | copy-start | bytes 7684
Sparse Core Ops, SparseCore 0:
  116.2 35.9 all-gather.3
